TPU v7x, 32 devices: a whole 2x2x4 slice. The times are simulated.
32 devices in a mesh: cp: 16 (over z, y, x), hd: 2 (over core).
Axes of the slice: x: 2, y: 2, z: 4, core: 2. Of those that a mesh axis runs over, the one named last changes fastest.
Arguments:
- queries: bfloat16 [3072, 4096], P('cp', 'hd'), may hold values from -48 to 48
- keys: bfloat16 [3072, 1024], P('cp', 'hd'), may hold values from -48 to 48
- values: bfloat16 [3072, 1024], P('cp', 'hd'), may hold values from -6 to 6
- span_table: int32 [32], replicated, may hold values from 0 to 31, as said below
- doc_ids: int32 [3072], replicated, may hold values from 0 to 7, never falling along the last dimension, each value on 1 to 768 neighbouring positions
- out_weight: bfloat16 [4096, 4096], P('hd'), may hold values from -0.09375 to 0.09375
Outputs:
- mixed: bfloat16 [3072, 4096], P(('cp', 'hd'))
Inputs may be any that keep to these rules, and one draw needn't show every extreme that they name: `span_table`: slots 2 j and 2 j + 1 hold two spans c and 31 - c, and every span is held once.
All inputs are finite; a program needn't handle non-finite values.
Results may differ from a plain program's by a relative error of at most 0.0095.
Values may be sent and summed in bfloat16 or wider, within the bound.
A program may use at most 128 MiB of HBM per device.

v0:
```python
import jax
import jax.numpy as jnp
from jax import lax
from jax.sharding import PartitionSpec as P

HEAD_WIDTH = 128


def local(queries, keys, values, span_table, doc_ids, out_weight):
    tok_rows = queries.shape[0]
    span_len = tok_rows // 2
    span_count = span_table.shape[0]
    local_heads = queries.shape[1] // HEAD_WIDTH
    kv_heads = keys.shape[1] // HEAD_WIDTH
    query_group = local_heads // kv_heads
    scale = HEAD_WIDTH ** (-0.5)
    slot_onehot = (span_table[:, None] == jnp.arange(span_count, dtype=jnp.int32)[None, :]).astype(
        jnp.float32
    )
    doc_by_span = doc_ids.reshape(span_count, span_len).astype(jnp.float32)
    held_doc = jnp.dot(
        slot_onehot,
        doc_by_span,
        precision=lax.Precision.HIGHEST,
        preferred_element_type=jnp.float32,
    )
    held_doc = held_doc.astype(jnp.int32).reshape(span_count * span_len)
    held_pos = span_table[:, None] * span_len + jnp.arange(span_len, dtype=jnp.int32)[None, :]
    held_pos = held_pos.reshape(span_count * span_len)

    def locate(first):
        place = lax.dynamic_slice_in_dim(held_pos, first, tok_rows, 0)
        document = lax.dynamic_slice_in_dim(held_doc, first, tok_rows, 0)
        return (place, document)

    query_pos, query_doc = locate(lax.axis_index("cp") * tok_rows)
    query_heads = queries.reshape(tok_rows, kv_heads, query_group, HEAD_WIDTH)

    def visit(carry, key_block, value_block, key_start):
        key_pos, key_doc = locate(key_start)
        visible = (key_pos[None, :] <= query_pos[:, None]) & (
            key_doc[None, :] == query_doc[:, None]
        )

        def update(state):
            best, total, accum = state
            key_head_rows = key_block.reshape(tok_rows, kv_heads, HEAD_WIDTH)
            value_head_rows = value_block.reshape(tok_rows, kv_heads, HEAD_WIDTH)
            scores = (
                jnp.einsum(
                    "qkgd,nkd->kgqn", query_heads, key_head_rows, preferred_element_type=jnp.float32
                )
                * scale
            )
            scores = jnp.where(visible, scores, -1e30)
            new_best = jnp.maximum(best, jnp.max(scores, axis=-1))
            weights = jnp.where(visible, jnp.exp(scores - new_best[..., None]), 0.0)
            fade = jnp.exp(best - new_best)
            total = total * fade + jnp.sum(weights, axis=-1)
            accum = accum * fade[..., None] + jnp.einsum(
                "kgqn,nkd->kgqd",
                weights.astype(jnp.bfloat16),
                value_head_rows,
                preferred_element_type=jnp.float32,
            )
            return (new_best, total, accum)

        return lax.cond(jnp.any(visible), update, lambda state: state, carry)

    init = (
        jnp.full((kv_heads, query_group, tok_rows), -1e30, jnp.float32),
        jnp.zeros((kv_heads, query_group, tok_rows), jnp.float32),
        jnp.zeros((kv_heads, query_group, tok_rows, HEAD_WIDTH), jnp.float32),
    )
    key_piece = lax.all_gather(keys, "cp", axis=0, tiled=True)
    value_piece = lax.all_gather(values, "cp", axis=0, tiled=True)
    count = key_piece.shape[0] // tok_rows

    def step(index, state):
        offset = (index * tok_rows).astype(jnp.int32)
        key_block = lax.dynamic_slice_in_dim(key_piece, offset, tok_rows, 0)
        value_block = lax.dynamic_slice_in_dim(value_piece, offset, tok_rows, 0)
        return visit(state, key_block, value_block, offset)

    best, total, accum = lax.fori_loop(0, count, step, init)
    attn = (
        (accum / total[..., None])
        .transpose(2, 0, 1, 3)
        .reshape(tok_rows, local_heads * HEAD_WIDTH)
        .astype(jnp.bfloat16)
    )
    return lax.psum_scatter(
        jnp.dot(attn, out_weight, preferred_element_type=jnp.float32).astype(jnp.bfloat16),
        "hd",
        scatter_dimension=0,
        tiled=True,
    )


def solution(mesh):
    return jax.shard_map(
        local,
        mesh=mesh,
        in_specs=(P("cp", "hd"), P("cp", "hd"), P("cp", "hd"), P(), P(), P("hd", None)),
        out_specs=P(("cp", "hd"), None),
        check_vma=False,
    )
```

profile of v0, /device:TPU:0, one launch (start us, length us, event | category | flops | bytes accessed | tf_op | source)
XLA Modules:
  0.0 240.0 jit_solution(14145306607009826491)
XLA Ops:
  8.8 0.8 convolution_convert_fusion.1
  10.7 2.3 reshape.35
  13.2 67.5 %all-gather.3.cloned.1.call-done = bf16[3072,512]{1,0:T(8,128)(2,1)} async-done(((bf16[192,512]{1,0:T(8,128)(2,1)}), bf16[3072,512]{1,0:T(8,128)(2,1)}) %all-gather.3.cloned.1.call-update) | async-done | bytes 3145744 | tf_op jit(solution)/shard_map/all_gather | solution.py:75
  80.7 69.2 %all-gather.5.cloned.1.call-done = bf16[3072,512]{1,0:T(8,128)(2,1)} async-done(((bf16[192,512]{1,0:T(8,128)(2,1)}), bf16[3072,512]{1,0:T(8,128)(2,1)}) %all-gather.5.cloned.1.call-update) | async-done | bytes 3145744 | tf_op jit(solution)/shard_map/all_gather | solution.py:76
  150.1 59.1 %while.17 = (s32[]{:T(128)}, f32[4,4,192]{2,1,0:T(4,128)S(1)}, f32[4,4,192]{2,1,0:T(4,128)S(1)}, f32[4,4,192,128]{3,2,1,0:T(8,128)S(1)}, s32[3072]{0:T(1024)S(1)...) while((s32[]{:T(128)}, f32[4,4,192]{2,1,0:T(4,128)S(1)}, ...), condition=%wide.region_6.7_spmd, body=%wide.region_0.6_spmd.sunk | while | flops 310597632 | bytes 13326661 | solution.py:85
  150.3 0.7 fusion.26
  151.6 4.4 %conditional.2 = ((f32[4,4,192]{2,1,0:T(4,128)S(1)}, f32[4,4,192]{2,1,0:T(4,128)S(1)}, f32[4,4,192,128]{3,2,1,0:T(8,128)S(1)})) conditional(s32[]{:T(128)} %convert_element_type.51, (f32[4,4,192]{2,1,0:T(4,128)S(1)}, f32[4,4,192]{2,1,0:T(4,128)S(1)}, f32[4,4,192,128]{3,2,1,0:T(8,128)S(1)}) %tuple.49, (pred[192,192]{0,1:T(8,128)(4,1)S(1)}, ...), branch_computations={%region_2.0_spmd, %region_3.5_spmd} | conditional | flops 310450176 | bytes 13283364 | solution.py:68
  151.6 1.1 constant_dynamic-slice_fusion
  152.7 0.7 fusion
  153.5 0.8 fusion.2
  154.4 1.6 multiply_add_fusion
  157.5 4.4 %conditional.2 = ((f32[4,4,192]{2,1,0:T(4,128)S(1)}, f32[4,4,192]{2,1,0:T(4,128)S(1)}, f32[4,4,192,128]{3,2,1,0:T(8,128)S(1)})) conditional(s32[]{:T(128)} %convert_element_type.51, (f32[4,4,192]{2,1,0:T(4,128)S(1)}, f32[4,4,192]{2,1,0:T(4,128)S(1)}, f32[4,4,192,128]{3,2,1,0:T(8,128)S(1)}) %tuple.49, (pred[192,192]{0,1:T(8,128)(4,1)S(1)}, ...), branch_computations={%region_2.0_spmd, %region_3.5_spmd} | conditional | flops 310450176 | bytes 13283364 | solution.py:68
  157.5 1.1 constant_dynamic-slice_fusion
  158.7 0.7 fusion
  159.4 0.8 fusion.2
  160.3 1.6 multiply_add_fusion
  163.4 4.4 %conditional.2 = ((f32[4,4,192]{2,1,0:T(4,128)S(1)}, f32[4,4,192]{2,1,0:T(4,128)S(1)}, f32[4,4,192,128]{3,2,1,0:T(8,128)S(1)})) conditional(s32[]{:T(128)} %convert_element_type.51, (f32[4,4,192]{2,1,0:T(4,128)S(1)}, f32[4,4,192]{2,1,0:T(4,128)S(1)}, f32[4,4,192,128]{3,2,1,0:T(8,128)S(1)}) %tuple.49, (pred[192,192]{0,1:T(8,128)(4,1)S(1)}, ...), branch_computations={%region_2.0_spmd, %region_3.5_spmd} | conditional | flops 310450176 | bytes 13283364 | solution.py:68
  163.4 1.1 constant_dynamic-slice_fusion
  164.6 0.7 fusion
  165.3 0.8 fusion.2
  166.2 1.6 multiply_add_fusion
  173.7 4.4 %conditional.2 = ((f32[4,4,192]{2,1,0:T(4,128)S(1)}, f32[4,4,192]{2,1,0:T(4,128)S(1)}, f32[4,4,192,128]{3,2,1,0:T(8,128)S(1)})) conditional(s32[]{:T(128)} %convert_element_type.51, (f32[4,4,192]{2,1,0:T(4,128)S(1)}, f32[4,4,192]{2,1,0:T(4,128)S(1)}, f32[4,4,192,128]{3,2,1,0:T(8,128)S(1)}) %tuple.49, (pred[192,192]{0,1:T(8,128)(4,1)S(1)}, ...), branch_computations={%region_2.0_spmd, %region_3.5_spmd} | conditional | flops 310450176 | bytes 13283364 | solution.py:68
  173.8 1.1 constant_dynamic-slice_fusion
  174.9 0.7 fusion
  175.7 0.8 fusion.2
  176.5 1.6 multiply_add_fusion
  179.7 4.4 %conditional.2 = ((f32[4,4,192]{2,1,0:T(4,128)S(1)}, f32[4,4,192]{2,1,0:T(4,128)S(1)}, f32[4,4,192,128]{3,2,1,0:T(8,128)S(1)})) conditional(s32[]{:T(128)} %convert_element_type.51, (f32[4,4,192]{2,1,0:T(4,128)S(1)}, f32[4,4,192]{2,1,0:T(4,128)S(1)}, f32[4,4,192,128]{3,2,1,0:T(8,128)S(1)}) %tuple.49, (pred[192,192]{0,1:T(8,128)(4,1)S(1)}, ...), branch_computations={%region_2.0_spmd, %region_3.5_spmd} | conditional | flops 310450176 | bytes 13283364 | solution.py:68
  179.7 1.1 constant_dynamic-slice_fusion
  180.8 0.7 fusion
  181.6 0.8 fusion.2
  182.4 1.6 multiply_add_fusion
  185.6 4.4 %conditional.2 = ((f32[4,4,192]{2,1,0:T(4,128)S(1)}, f32[4,4,192]{2,1,0:T(4,128)S(1)}, f32[4,4,192,128]{3,2,1,0:T(8,128)S(1)})) conditional(s32[]{:T(128)} %convert_element_type.51, (f32[4,4,192]{2,1,0:T(4,128)S(1)}, f32[4,4,192]{2,1,0:T(4,128)S(1)}, f32[4,4,192,128]{3,2,1,0:T(8,128)S(1)}) %tuple.49, (pred[192,192]{0,1:T(8,128)(4,1)S(1)}, ...), branch_computations={%region_2.0_spmd, %region_3.5_spmd} | conditional | flops 310450176 | bytes 13283364 | solution.py:68
  185.6 1.1 constant_dynamic-slice_fusion
  186.7 0.7 fusion
  187.5 0.8 fusion.2
  188.4 1.6 multiply_add_fusion
  195.9 4.4 %conditional.2 = ((f32[4,4,192]{2,1,0:T(4,128)S(1)}, f32[4,4,192]{2,1,0:T(4,128)S(1)}, f32[4,4,192,128]{3,2,1,0:T(8,128)S(1)})) conditional(s32[]{:T(128)} %convert_element_type.51, (f32[4,4,192]{2,1,0:T(4,128)S(1)}, f32[4,4,192]{2,1,0:T(4,128)S(1)}, f32[4,4,192,128]{3,2,1,0:T(8,128)S(1)}) %tuple.49, (pred[192,192]{0,1:T(8,128)(4,1)S(1)}, ...), branch_computations={%region_2.0_spmd, %region_3.5_spmd} | conditional | flops 310450176 | bytes 13283364 | solution.py:68
  195.9 1.1 constant_dynamic-slice_fusion
  197.1 0.7 fusion
  197.9 0.8 fusion.2
  198.7 1.6 multiply_add_fusion
  201.8 4.4 %conditional.2 = ((f32[4,4,192]{2,1,0:T(4,128)S(1)}, f32[4,4,192]{2,1,0:T(4,128)S(1)}, f32[4,4,192,128]{3,2,1,0:T(8,128)S(1)})) conditional(s32[]{:T(128)} %convert_element_type.51, (f32[4,4,192]{2,1,0:T(4,128)S(1)}, f32[4,4,192]{2,1,0:T(4,128)S(1)}, f32[4,4,192,128]{3,2,1,0:T(8,128)S(1)}) %tuple.49, (pred[192,192]{0,1:T(8,128)(4,1)S(1)}, ...), branch_computations={%region_2.0_spmd, %region_3.5_spmd} | conditional | flops 310450176 | bytes 13283364 | solution.py:68
  201.8 1.1 constant_dynamic-slice_fusion
  203.0 0.7 fusion
  203.8 0.8 fusion.2
  204.6 1.6 multiply_add_fusion
  211.0 10.4 %convolution_convert_fusion = bf16[192,4096]{1,0:T(8,128)(2,1)} fusion(bf16[192,2048]{1,0:T(8,128)(2,1)S(1)} %convert_element_type.39, bf16[2048,4096]{1,0:T(8,128)(2,1)} %param.15), kind=kOutput, calls=%fused_computation.23 | convolution fusion | flops 3222011904 | bytes 19136512 | tf_op jit(solution)/shard_map/dot_general | solution.py:93
  221.3 12.2 %reduce-scatter.2.cloned.1.call-done = bf16[96,4096]{1,0:T(8,128)(2,1)} async-done(((bf16[192,4096]{1,0:T(8,128)(2,1)}), bf16[96,4096]{1,0:T(8,128)(2,1)}) %reduce-scatter.2.cloned.1.call-update) | async-done | bytes 786448 | tf_op jit(solution)/shard_map/reduce_scatter | solution.py:92
  (116 shorter events, 19.9 us)
Async XLA Ops:
  6.5 74.2 %all-gather.3.cloned.1.call-start = ((), (), s32[]{:S(2)}) async-start(), calls=%async_computation.1 | async-start | bytes 3342336 | tf_op jit(solution)/shard_map/all_gather | solution.py:75
  7.3 142.7 %all-gather.5.cloned.1.call-start = ((), (), s32[]{:S(2)}) async-start(), calls=%async_computation.2 | async-start | bytes 3342336 | tf_op jit(solution)/shard_map/all_gather | solution.py:76
  8.0 225.5 %reduce-scatter.2.cloned.1.call-start = ((), (), s32[]{:S(2)}) async-start(), calls=%async_computation.3 | async-start | bytes 2359296 | tf_op jit(solution)/shard_map/reduce_scatter | solution.py:92
Sparse Core Ops, SparseCore 0:
  10.1 70.5 all-gather.2
  83.5 66.3 all-gather.4
  221.5 11.9 reduce-scatter.1
where the time goes:
time: 241 us; the launch traced here: 240 us
  waiting for transfers between devices  150 us (62%)
  matrix products  30.1 us (12%)
  other arithmetic  20.4 us (8%)
  local copies, waits for them, and re-layouts  16 us (7%)
  between operations  13.2 us (5%)
  loops' own time  9.95 us (4%)
    all_gather x1, waiting for transfers between devices, local(): value_piece = lax.all_gather(values, 'cp', axis=0, tiled=True)  69.2 us
    all_gather x1, waiting for transfers between devices, local(): key_piece = lax.all_gather(keys, 'cp', axis=0, tiled=True)  67.5 us
    dot_general x8, matrix products, update(): jnp.einsum('kgqn,nkd->kgqd', weights.astype(jnp.bfloat16), value_head_row...  13.1 us
    reduce_scatter x1, waiting for transfers between devices, local(): lax.psum_scatter(jnp.dot(attn, out_weight, preferred_element_type=jnp.flo...  12.2 us
    reduce_or x16, other arithmetic, visit(): return lax.cond(jnp.any(visible), update, lambda state: state, carry)  11.6 us
    dot_general x1, matrix products, local(): jnp.dot(attn, out_weight, preferred_element_type=jnp.float32)  10.4 us
    another operation x1, loops' own time, local(): best, total, accum = lax.fori_loop(0, count, step, init)  9.39 us
    dynamic_slice x8, local copies, waits for them, and re-layouts, step(): value_block = lax.dynamic_slice_in_dim(value_piece, offset, tok_rows, 0)  8.44 us
  transfers between devices with their start and end apart: 3, of which 3 were waited for; matrix products, arithmetic and copies ran while one was open for 2% of the time, Pallas kernels for 0%

commit v1 on v0

--- a/solution.py
+++ b/solution.py
@@ -4,6 +4,24 @@
 from jax.sharding import PartitionSpec as P
 
 HEAD_WIDTH = 128
+
+
+def cover_the_node(mat):
+    row_list = [mat]
+    num_devices = lax.axis_size("cp")
+    hop_no = 0
+    while hop_no < num_devices - 1:
+        row_list.append(
+            lax.ppermute(
+                row_list[-1],
+                "cp",
+                [(dev_j, (dev_j + 1) % num_devices) for dev_j in range(num_devices)],
+            )
+        )
+        hop_no = hop_no + 1
+    return jnp.roll(
+        jnp.concatenate(row_list[::-1], axis=0), (lax.axis_index("cp") + 1) * mat.shape[0], axis=0
+    )
 
 
 def local(queries, keys, values, span_table, doc_ids, out_weight):
@@ -73,7 +91,7 @@
         jnp.zeros((kv_heads, query_group, tok_rows, HEAD_WIDTH), jnp.float32),
     )
     key_piece = lax.all_gather(keys, "cp", axis=0, tiled=True)
-    value_piece = lax.all_gather(values, "cp", axis=0, tiled=True)
+    value_piece = cover_the_node(values)
     count = key_piece.shape[0] // tok_rows
 
     def step(index, state):

time: 241 us -> 360 us (1.49)
  local copies, waits for them, and re-layouts: 16 us -> 60.2 us
  other arithmetic: 20.4 us -> 55 us
  matrix products: 30.1 us -> 53.9 us
  waiting for transfers between devices: 150 us -> 160 us
    ppermute x0 -> x15, waiting for transfers between devices: none -> 148 us  [cover_the_node(): lax.ppermute(row_list[-1], 'cp', [(dev_j, (dev_j + 1) % num_devices) for...]
    all_gather x1 -> x0, waiting for transfers between devices: 69.2 us -> none  [local(): value_piece = lax.all_gather(values, 'cp', axis=0, tiled=True)]
    all_gather x1, waiting for transfers between devices: 67.5 us -> 0.01 us  [local(): key_piece = lax.all_gather(keys, 'cp', axis=0, tiled=True)]
    reduce_or x16, other arithmetic: 11.6 us -> 33.8 us  [visit(): return lax.cond(jnp.any(visible), update, lambda state: state, carry)]
    dot_general x8, matrix products: 13.1 us -> 27.9 us  [update(): jnp.einsum('kgqn,nkd->kgqd', weights.astype(jnp.bfloat16), value_head_row...]
    dynamic_slice x17, local copies, waits for them, and re-layouts: 1.37 us -> 13.8 us  [locate(): document = lax.dynamic_slice_in_dim(held_doc, first, tok_rows, 0)]
    dynamic_slice x17, local copies, waits for them, and re-layouts: 1.28 us -> 13.5 us  [locate(): place = lax.dynamic_slice_in_dim(held_pos, first, tok_rows, 0)]
    cond x8 -> x72, local copies, waits for them, and re-layouts: 0.03 us -> 9.63 us
  transfers between devices with their start and end apart: 3 -> 17, of which waited for: 3 -> 16; matrix products, arithmetic and copies ran while one was open for 2% -> 5% of each run, Pallas kernels for 0% -> 0%
where the time goes in v1:
time: 360 us; the launch traced here: 357 us
  waiting for transfers between devices  160 us (44%)
  local copies, waits for them, and re-layouts  60.2 us (17%)
  other arithmetic  55 us (15%)
  matrix products  53.9 us (15%)
  between operations  13.7 us (4%)
  loops' own time  11.2 us (3%)
    ppermute x15, waiting for transfers between devices, cover_the_node(): lax.ppermute(row_list[-1], 'cp', [(dev_j, (dev_j + 1) % num_devices) for...  148 us
    reduce_or x16, other arithmetic, visit(): return lax.cond(jnp.any(visible), update, lambda state: state, carry)  33.8 us
    dot_general x8, matrix products, update(): jnp.einsum('kgqn,nkd->kgqd', weights.astype(jnp.bfloat16), value_head_row...  27.9 us
    dot_general x8, matrix products, update(): jnp.einsum('qkgd,nkd->kgqn', query_heads, key_head_rows, preferred_elemen...  14.9 us
    dynamic_slice x17, local copies, waits for them, and re-layouts, locate(): document = lax.dynamic_slice_in_dim(held_doc, first, tok_rows, 0)  13.8 us
    dynamic_slice x17, local copies, waits for them, and re-layouts, locate(): place = lax.dynamic_slice_in_dim(held_pos, first, tok_rows, 0)  13.5 us
    reduce_sum x8, other arithmetic, update(): total = total * fade + jnp.sum(weights, axis=-1)  12.9 us
    reduce_scatter x1, waiting for transfers between devices, local(): lax.psum_scatter(jnp.dot(attn, out_weight, preferred_element_type=jnp.flo...  12.2 us
  transfers between devices with their start and end apart: 17, of which 16 were waited for; matrix products, arithmetic and copies ran while one was open for 5% of the time, Pallas kernels for 0%

profile of v1, /device:TPU:0, one launch (start us, length us, event | category | flops | bytes accessed | tf_op | source)
XLA Modules:
  0.0 357.3 jit_solution(17001830091705366998)
XLA Ops:
  6.5 3.0 collective-permute-start
  9.5 9.2 %collective-permute-done = bf16[192,512]{1,0:T(8,128)(2,1)S(1)} collective-permute-done((bf16[192,512]{1,0:T(8,128)(2,1)}, bf16[192,512]{1,0:T(8,128)(2,1)S(1)}, u32[]{:S(2)}, u32[]{:S(2)}) %collective-permute-start) | collective-permute-done | bytes 196640 | tf_op jit(solution)/shard_map/ppermute | solution.py:15
  18.7 9.7 %collective-permute-done.1 = bf16[192,512]{1,0:T(8,128)(2,1)S(1)} collective-permute-done((bf16[192,512]{1,0:T(8,128)(2,1)S(1)}, bf16[192,512]{1,0:T(8,128)(2,1)S(1)}, u32[]{:S(2)}, u32[]{:S(2)}) %collective-permute-start.1) | collective-permute-done | bytes 196640 | tf_op jit(solution)/shard_map/ppermute | solution.py:15
  28.3 9.3 %collective-permute-done.2 = bf16[192,512]{1,0:T(8,128)(2,1)S(1)} collective-permute-done((bf16[192,512]{1,0:T(8,128)(2,1)S(1)}, bf16[192,512]{1,0:T(8,128)(2,1)S(1)}, u32[]{:S(2)}, u32[]{:S(2)}) %collective-permute-start.2) | collective-permute-done | bytes 196640 | tf_op jit(solution)/shard_map/ppermute | solution.py:15
  37.6 9.3 %collective-permute-done.3 = bf16[192,512]{1,0:T(8,128)(2,1)S(1)} collective-permute-done((bf16[192,512]{1,0:T(8,128)(2,1)S(1)}, bf16[192,512]{1,0:T(8,128)(2,1)S(1)}, u32[]{:S(2)}, u32[]{:S(2)}) %collective-permute-start.3) | collective-permute-done | bytes 196640 | tf_op jit(solution)/shard_map/ppermute | solution.py:15
  46.9 9.3 %collective-permute-done.4 = bf16[192,512]{1,0:T(8,128)(2,1)S(1)} collective-permute-done((bf16[192,512]{1,0:T(8,128)(2,1)S(1)}, bf16[192,512]{1,0:T(8,128)(2,1)S(1)}, u32[]{:S(2)}, u32[]{:S(2)}) %collective-permute-start.4) | collective-permute-done | bytes 196640 | tf_op jit(solution)/shard_map/ppermute | solution.py:15
  56.1 9.3 %collective-permute-done.5 = bf16[192,512]{1,0:T(8,128)(2,1)S(1)} collective-permute-done((bf16[192,512]{1,0:T(8,128)(2,1)S(1)}, bf16[192,512]{1,0:T(8,128)(2,1)S(1)}, u32[]{:S(2)}, u32[]{:S(2)}) %collective-permute-start.5) | collective-permute-done | bytes 196640 | tf_op jit(solution)/shard_map/ppermute | solution.py:15
  65.5 10.3 %collective-permute-done.6 = bf16[192,512]{1,0:T(8,128)(2,1)S(1)} collective-permute-done((bf16[192,512]{1,0:T(8,128)(2,1)S(1)}, bf16[192,512]{1,0:T(8,128)(2,1)S(1)}, u32[]{:S(2)}, u32[]{:S(2)}) %collective-permute-start.6) | collective-permute-done | bytes 196640 | tf_op jit(solution)/shard_map/ppermute | solution.py:15
  75.8 14.2 %collective-permute-done.7 = bf16[192,512]{1,0:T(8,128)(2,1)S(1)} collective-permute-done((bf16[192,512]{1,0:T(8,128)(2,1)S(1)}, bf16[192,512]{1,0:T(8,128)(2,1)S(1)}, u32[]{:S(2)}, u32[]{:S(2)}) %collective-permute-start.7) | collective-permute-done | bytes 196640 | tf_op jit(solution)/shard_map/ppermute | solution.py:15
  90.0 11.6 %collective-permute-done.8 = bf16[192,512]{1,0:T(8,128)(2,1)S(1)} collective-permute-done((bf16[192,512]{1,0:T(8,128)(2,1)S(1)}, bf16[192,512]{1,0:T(8,128)(2,1)S(1)}, u32[]{:S(2)}, u32[]{:S(2)}) %collective-permute-start.8) | collective-permute-done | bytes 196640 | tf_op jit(solution)/shard_map/ppermute | solution.py:15
  101.7 11.8 %collective-permute-done.9 = bf16[192,512]{1,0:T(8,128)(2,1)S(1)} collective-permute-done((bf16[192,512]{1,0:T(8,128)(2,1)S(1)}, bf16[192,512]{1,0:T(8,128)(2,1)S(1)}, u32[]{:S(2)}, u32[]{:S(2)}) %collective-permute-start.9) | collective-permute-done | bytes 196640 | tf_op jit(solution)/shard_map/ppermute | solution.py:15
  113.4 11.2 %collective-permute-done.10 = bf16[192,512]{1,0:T(8,128)(2,1)S(1)} collective-permute-done((bf16[192,512]{1,0:T(8,128)(2,1)S(1)}, bf16[192,512]{1,0:T(8,128)(2,1)S(1)}, u32[]{:S(2)}, u32[]{:S(2)}) %collective-permute-start.10) | collective-permute-done | bytes 196640 | tf_op jit(solution)/shard_map/ppermute | solution.py:15
  125.4 13.8 %collective-permute-done.11 = bf16[192,512]{1,0:T(8,128)(2,1)S(1)} collective-permute-done((bf16[192,512]{1,0:T(8,128)(2,1)S(1)}, bf16[192,512]{1,0:T(8,128)(2,1)S(1)}, u32[]{:S(2)}, u32[]{:S(2)}) %collective-permute-start.11) | collective-permute-done | bytes 196640 | tf_op jit(solution)/shard_map/ppermute | solution.py:15
  140.8 7.7 %collective-permute-done.12 = bf16[192,512]{1,0:T(8,128)(2,1)S(1)} collective-permute-done((bf16[192,512]{1,0:T(8,128)(2,1)S(1)}, bf16[192,512]{1,0:T(8,128)(2,1)S(1)}, u32[]{:S(2)}, u32[]{:S(2)}) %collective-permute-start.12) | collective-permute-done | bytes 196640 | tf_op jit(solution)/shard_map/ppermute | solution.py:15
  149.1 8.7 %collective-permute-done.13 = bf16[192,512]{1,0:T(8,128)(2,1)} collective-permute-done((bf16[192,512]{1,0:T(8,128)(2,1)S(1)}, bf16[192,512]{1,0:T(8,128)(2,1)}, u32[]{:S(2)}, u32[]{:S(2)}) %collective-permute-start.13) | collective-permute-done | bytes 196640 | tf_op jit(solution)/shard_map/ppermute | solution.py:15
  161.3 2.3 reshape.35
  164.7 2.7 collective-permute-done.14
  171.9 2.5 constant_dynamic-slice_fusion.2
  175.7 149.1 %while.17 = (s32[]{:T(128)}, f32[4,4,192]{2,1,0:T(4,128)S(1)}, f32[4,4,192]{2,1,0:T(4,128)S(1)}, f32[4,4,192,128]{3,2,1,0:T(8,128)}, s32[3072]{0:T(1024)}, /*ind...) while((s32[]{:T(128)}, f32[4,4,192]{2,1,0:T(4,128)S(1)}, ...), condition=%wide.region_6.7_spmd, body=%wide.region_0.6_spmd.sunk | while | flops 310597632 | bytes 13523381 | solution.py:103
  177.2 2.1 fusion.26
  179.9 10.0 %conditional.2 = ((f32[4,4,192]{2,1,0:T(4,128)S(1)}, f32[4,4,192]{2,1,0:T(4,128)S(1)}, f32[4,4,192,128]{3,2,1,0:T(8,128)})) conditional(s32[]{:T(128)} %convert_element_type.51, (f32[4,4,192]{2,1,0:T(4,128)S(1)}, f32[4,4,192]{2,1,0:T(4,128)S(1)}, f32[4,4,192,128]{3,2,1,0:T(8,128)}) %tuple.49, (pred[192,192]{0,1:T(8,128)(4,1)}, ...), branch_computations={%region_2.2_spmd, %region_3.5_spmd} | conditional | flops 310450176 | bytes 13480084 | solution.py:86
  186.5 3.5 multiply_add_fusion
  194.3 10.0 %conditional.2 = ((f32[4,4,192]{2,1,0:T(4,128)S(1)}, f32[4,4,192]{2,1,0:T(4,128)S(1)}, f32[4,4,192,128]{3,2,1,0:T(8,128)})) conditional(s32[]{:T(128)} %convert_element_type.51, (f32[4,4,192]{2,1,0:T(4,128)S(1)}, f32[4,4,192]{2,1,0:T(4,128)S(1)}, f32[4,4,192,128]{3,2,1,0:T(8,128)}) %tuple.49, (pred[192,192]{0,1:T(8,128)(4,1)}, ...), branch_computations={%region_2.2_spmd, %region_3.5_spmd} | conditional | flops 310450176 | bytes 13480084 | solution.py:86
  200.8 3.5 multiply_add_fusion
  205.9 2.1 fusion.26
  208.6 10.0 %conditional.2 = ((f32[4,4,192]{2,1,0:T(4,128)S(1)}, f32[4,4,192]{2,1,0:T(4,128)S(1)}, f32[4,4,192,128]{3,2,1,0:T(8,128)})) conditional(s32[]{:T(128)} %convert_element_type.51, (f32[4,4,192]{2,1,0:T(4,128)S(1)}, f32[4,4,192]{2,1,0:T(4,128)S(1)}, f32[4,4,192,128]{3,2,1,0:T(8,128)}) %tuple.49, (pred[192,192]{0,1:T(8,128)(4,1)}, ...), branch_computations={%region_2.2_spmd, %region_3.5_spmd} | conditional | flops 310450176 | bytes 13480084 | solution.py:86
  215.1 3.5 multiply_add_fusion
  224.5 2.1 fusion.26
  228.8 2.1 fusion.26
  235.9 10.0 %conditional.2 = ((f32[4,4,192]{2,1,0:T(4,128)S(1)}, f32[4,4,192]{2,1,0:T(4,128)S(1)}, f32[4,4,192,128]{3,2,1,0:T(8,128)})) conditional(s32[]{:T(128)} %convert_element_type.51, (f32[4,4,192]{2,1,0:T(4,128)S(1)}, f32[4,4,192]{2,1,0:T(4,128)S(1)}, f32[4,4,192,128]{3,2,1,0:T(8,128)}) %tuple.49, (pred[192,192]{0,1:T(8,128)(4,1)}, ...), branch_computations={%region_2.2_spmd, %region_3.5_spmd} | conditional | flops 310450176 | bytes 13480084 | solution.py:86
  242.4 3.5 multiply_add_fusion
  247.5 2.1 fusion.26
  250.3 10.0 %conditional.2 = ((f32[4,4,192]{2,1,0:T(4,128)S(1)}, f32[4,4,192]{2,1,0:T(4,128)S(1)}, f32[4,4,192,128]{3,2,1,0:T(8,128)})) conditional(s32[]{:T(128)} %convert_element_type.51, (f32[4,4,192]{2,1,0:T(4,128)S(1)}, f32[4,4,192]{2,1,0:T(4,128)S(1)}, f32[4,4,192,128]{3,2,1,0:T(8,128)}) %tuple.49, (pred[192,192]{0,1:T(8,128)(4,1)}, ...), branch_computations={%region_2.2_spmd, %region_3.5_spmd} | conditional | flops 310450176 | bytes 13480084 | solution.py:86
  256.8 3.5 multiply_add_fusion
  261.9 2.1 fusion.26
  264.6 10.0 %conditional.2 = ((f32[4,4,192]{2,1,0:T(4,128)S(1)}, f32[4,4,192]{2,1,0:T(4,128)S(1)}, f32[4,4,192,128]{3,2,1,0:T(8,128)})) conditional(s32[]{:T(128)} %convert_element_type.51, (f32[4,4,192]{2,1,0:T(4,128)S(1)}, f32[4,4,192]{2,1,0:T(4,128)S(1)}, f32[4,4,192,128]{3,2,1,0:T(8,128)}) %tuple.49, (pred[192,192]{0,1:T(8,128)(4,1)}, ...), branch_computations={%region_2.2_spmd, %region_3.5_spmd} | conditional | flops 310450176 | bytes 13480084 | solution.py:86
  271.1 3.5 multiply_add_fusion
  276.2 2.1 fusion.26
  284.9 2.1 fusion.26
  291.9 10.0 %conditional.2 = ((f32[4,4,192]{2,1,0:T(4,128)S(1)}, f32[4,4,192]{2,1,0:T(4,128)S(1)}, f32[4,4,192,128]{3,2,1,0:T(8,128)})) conditional(s32[]{:T(128)} %convert_element_type.51, (f32[4,4,192]{2,1,0:T(4,128)S(1)}, f32[4,4,192]{2,1,0:T(4,128)S(1)}, f32[4,4,192,128]{3,2,1,0:T(8,128)}) %tuple.49, (pred[192,192]{0,1:T(8,128)(4,1)}, ...), branch_computations={%region_2.2_spmd, %region_3.5_spmd} | conditional | flops 310450176 | bytes 13480084 | solution.py:86
  298.4 3.5 multiply_add_fusion
  303.4 2.1 fusion.26
  306.2 10.0 %conditional.2 = ((f32[4,4,192]{2,1,0:T(4,128)S(1)}, f32[4,4,192]{2,1,0:T(4,128)S(1)}, f32[4,4,192,128]{3,2,1,0:T(8,128)})) conditional(s32[]{:T(128)} %convert_element_type.51, (f32[4,4,192]{2,1,0:T(4,128)S(1)}, f32[4,4,192]{2,1,0:T(4,128)S(1)}, f32[4,4,192,128]{3,2,1,0:T(8,128)}) %tuple.49, (pred[192,192]{0,1:T(8,128)(4,1)}, ...), branch_computations={%region_2.2_spmd, %region_3.5_spmd} | conditional | flops 310450176 | bytes 13480084 | solution.py:86
  312.7 3.5 multiply_add_fusion
  317.7 2.1 fusion.26
  322.0 2.1 fusion.26
  327.9 10.4 %convolution_convert_fusion = bf16[192,4096]{1,0:T(8,128)(2,1)} fusion(bf16[192,2048]{1,0:T(8,128)(2,1)S(1)} %convert_element_type.39, bf16[2048,4096]{1,0:T(8,128)(2,1)} %param.15), kind=kOutput, calls=%fused_computation.23 | convolution fusion | flops 3222011904 | bytes 19136512 | tf_op jit(solution)/shard_map/dot_general | solution.py:111
  338.2 12.2 %reduce-scatter.2.cloned.1.call-done = bf16[96,4096]{1,0:T(8,128)(2,1)} async-done(((bf16[192,4096]{1,0:T(8,128)(2,1)}), bf16[96,4096]{1,0:T(8,128)(2,1)}) %reduce-scatter.2.cloned.1.call-update) | async-done | bytes 786448 | tf_op jit(solution)/shard_map/reduce_scatter | solution.py:110
  (242 shorter events, 103.1 us)
Async XLA Ops:
  6.5 163.1 %copy-start.4 = (bf16[192,512]{1,0:T(8,128)(2,1)S(1)}, bf16[192,512]{1,0:T(8,128)(2,1)}, u32[]{:S(2)}) copy-start(bf16[192,512]{1,0:T(8,128)(2,1)} %param.12) | copy-start | bytes 589828
  6.5 167.8 %all-gather.2.cloned.1.call-start = ((), (), s32[]{:S(2)}) async-start(), calls=%async_computation.1 | async-start | bytes 3342336 | tf_op jit(solution)/shard_map/all_gather | solution.py:93
  6.5 12.1 %collective-permute-start = (bf16[192,512]{1,0:T(8,128)(2,1)}, bf16[192,512]{1,0:T(8,128)(2,1)S(1)}, u32[]{:S(2)}, u32[]{:S(2)}) collective-permute-start(bf16[192,512]{1,0:T(8,128)(2,1)} %param.12), channel_id=1, source_target_pairs={{0,2},{2,4},{4,6},{6,8},{8,10},{10,12},{12,14},{14,16},{16,18},{18... | collective-permute-start | bytes 589832 | tf_op jit(solution)/shard_map/ppermute | solution.py:15
  18.7 9.7 %collective-permute-start.1 = (bf16[192,512]{1,0:T(8,128)(2,1)S(1)}, bf16[192,512]{1,0:T(8,128)(2,1)S(1)}, u32[]{:S(2)}, u32[]{:S(2)}) collective-permute-start(bf16[192,512]{1,0:T(8,128)(2,1)S(1)} %collective-permute-done), channel_id=1, source_target_pairs={{0,2},{2,4},{4,6},{6,8},{8,10},{10,12},{12,14},{14,16},{16,18},{18... | collective-permute-start | bytes 589832 | tf_op jit(solution)/shard_map/ppermute | solution.py:15
  28.3 9.3 %collective-permute-start.2 = (bf16[192,512]{1,0:T(8,128)(2,1)S(1)}, bf16[192,512]{1,0:T(8,128)(2,1)S(1)}, u32[]{:S(2)}, u32[]{:S(2)}) collective-permute-start(bf16[192,512]{1,0:T(8,128)(2,1)S(1)} %collective-permute-done.1), channel_id=1, source_target_pairs={{0,2},{2,4},{4,6},{6,8},{8,10},{10,12},{12,14},{14,16},{16,18},{18... | collective-permute-start | bytes 589832 | tf_op jit(solution)/shard_map/ppermute | solution.py:15
  37.6 9.3 %collective-permute-start.3 = (bf16[192,512]{1,0:T(8,128)(2,1)S(1)}, bf16[192,512]{1,0:T(8,128)(2,1)S(1)}, u32[]{:S(2)}, u32[]{:S(2)}) collective-permute-start(bf16[192,512]{1,0:T(8,128)(2,1)S(1)} %collective-permute-done.2), channel_id=1, source_target_pairs={{0,2},{2,4},{4,6},{6,8},{8,10},{10,12},{12,14},{14,16},{16,18},{18... | collective-permute-start | bytes 589832 | tf_op jit(solution)/shard_map/ppermute | solution.py:15
  46.9 9.3 %collective-permute-start.4 = (bf16[192,512]{1,0:T(8,128)(2,1)S(1)}, bf16[192,512]{1,0:T(8,128)(2,1)S(1)}, u32[]{:S(2)}, u32[]{:S(2)}) collective-permute-start(bf16[192,512]{1,0:T(8,128)(2,1)S(1)} %collective-permute-done.3), channel_id=1, source_target_pairs={{0,2},{2,4},{4,6},{6,8},{8,10},{10,12},{12,14},{14,16},{16,18},{18... | collective-permute-start | bytes 589832 | tf_op jit(solution)/shard_map/ppermute | solution.py:15
  56.1 9.3 %collective-permute-start.5 = (bf16[192,512]{1,0:T(8,128)(2,1)S(1)}, bf16[192,512]{1,0:T(8,128)(2,1)S(1)}, u32[]{:S(2)}, u32[]{:S(2)}) collective-permute-start(bf16[192,512]{1,0:T(8,128)(2,1)S(1)} %collective-permute-done.4), channel_id=1, source_target_pairs={{0,2},{2,4},{4,6},{6,8},{8,10},{10,12},{12,14},{14,16},{16,18},{18... | collective-permute-start | bytes 589832 | tf_op jit(solution)/shard_map/ppermute | solution.py:15
  65.4 10.4 %collective-permute-start.6 = (bf16[192,512]{1,0:T(8,128)(2,1)S(1)}, bf16[192,512]{1,0:T(8,128)(2,1)S(1)}, u32[]{:S(2)}, u32[]{:S(2)}) collective-permute-start(bf16[192,512]{1,0:T(8,128)(2,1)S(1)} %collective-permute-done.5), channel_id=1, source_target_pairs={{0,2},{2,4},{4,6},{6,8},{8,10},{10,12},{12,14},{14,16},{16,18},{18... | collective-permute-start | bytes 589832 | tf_op jit(solution)/shard_map/ppermute | solution.py:15
  65.4 285.0 %reduce-scatter.2.cloned.1.call-start = ((), (), s32[]{:S(2)}) async-start(), calls=%async_computation.2 | async-start | bytes 2359296 | tf_op jit(solution)/shard_map/reduce_scatter | solution.py:110
  75.8 14.2 %collective-permute-start.7 = (bf16[192,512]{1,0:T(8,128)(2,1)S(1)}, bf16[192,512]{1,0:T(8,128)(2,1)S(1)}, u32[]{:S(2)}, u32[]{:S(2)}) collective-permute-start(bf16[192,512]{1,0:T(8,128)(2,1)S(1)} %collective-permute-done.6), channel_id=1, source_target_pairs={{0,2},{2,4},{4,6},{6,8},{8,10},{10,12},{12,14},{14,16},{16,18},{18... | collective-permute-start | bytes 589832 | tf_op jit(solution)/shard_map/ppermute | solution.py:15
  90.0 11.6 %collective-permute-start.8 = (bf16[192,512]{1,0:T(8,128)(2,1)S(1)}, bf16[192,512]{1,0:T(8,128)(2,1)S(1)}, u32[]{:S(2)}, u32[]{:S(2)}) collective-permute-start(bf16[192,512]{1,0:T(8,128)(2,1)S(1)} %collective-permute-done.7), channel_id=1, source_target_pairs={{0,2},{2,4},{4,6},{6,8},{8,10},{10,12},{12,14},{14,16},{16,18},{18... | collective-permute-start | bytes 589832 | tf_op jit(solution)/shard_map/ppermute | solution.py:15
  101.6 11.8 %collective-permute-start.9 = (bf16[192,512]{1,0:T(8,128)(2,1)S(1)}, bf16[192,512]{1,0:T(8,128)(2,1)S(1)}, u32[]{:S(2)}, u32[]{:S(2)}) collective-permute-start(bf16[192,512]{1,0:T(8,128)(2,1)S(1)} %collective-permute-done.8), channel_id=1, source_target_pairs={{0,2},{2,4},{4,6},{6,8},{8,10},{10,12},{12,14},{14,16},{16,18},{18... | collective-permute-start | bytes 589832 | tf_op jit(solution)/shard_map/ppermute | solution.py:15
  113.4 11.2 %collective-permute-start.10 = (bf16[192,512]{1,0:T(8,128)(2,1)S(1)}, bf16[192,512]{1,0:T(8,128)(2,1)S(1)}, u32[]{:S(2)}, u32[]{:S(2)}) collective-permute-start(bf16[192,512]{1,0:T(8,128)(2,1)S(1)} %collective-permute-done.9), channel_id=1, source_target_pairs={{0,2},{2,4},{4,6},{6,8},{8,10},{10,12},{12,14},{14,16},{16,18},{18... | collective-permute-start | bytes 589832 | tf_op jit(solution)/shard_map/ppermute | solution.py:15
  124.6 14.6 %collective-permute-start.11 = (bf16[192,512]{1,0:T(8,128)(2,1)S(1)}, bf16[192,512]{1,0:T(8,128)(2,1)S(1)}, u32[]{:S(2)}, u32[]{:S(2)}) collective-permute-start(bf16[192,512]{1,0:T(8,128)(2,1)S(1)} %collective-permute-done.10), channel_id=1, source_target_pairs={{0,2},{2,4},{4,6},{6,8},{8,10},{10,12},{12,14},{14,16},{16,18},{18... | collective-permute-start | bytes 589832 | tf_op jit(solution)/shard_map/ppermute | solution.py:15
  139.2 9.3 %collective-permute-start.12 = (bf16[192,512]{1,0:T(8,128)(2,1)S(1)}, bf16[192,512]{1,0:T(8,128)(2,1)S(1)}, u32[]{:S(2)}, u32[]{:S(2)}) collective-permute-start(bf16[192,512]{1,0:T(8,128)(2,1)S(1)} %collective-permute-done.11), channel_id=1, source_target_pairs={{0,2},{2,4},{4,6},{6,8},{8,10},{10,12},{12,14},{14,16},{16,18},{18... | collective-permute-start | bytes 589832 | tf_op jit(solution)/shard_map/ppermute | solution.py:15
  148.5 9.4 %collective-permute-start.13 = (bf16[192,512]{1,0:T(8,128)(2,1)S(1)}, bf16[192,512]{1,0:T(8,128)(2,1)}, u32[]{:S(2)}, u32[]{:S(2)}) collective-permute-start(bf16[192,512]{1,0:T(8,128)(2,1)S(1)} %collective-permute-done.12), channel_id=1, source_target_pairs={{0,2},{2,4},{4,6},{6,8},{8,10},{10,12},{12,14},{14,16},{16,18},{18... | collective-permute-start | bytes 589832 | tf_op jit(solution)/shard_map/ppermute | solution.py:15
  157.8 9.6 %collective-permute-start.14 = (bf16[192,512]{1,0:T(8,128)(2,1)}, bf16[192,512]{1,0:T(8,128)(2,1)}, u32[]{:S(2)}, u32[]{:S(2)}) collective-permute-start(bf16[192,512]{1,0:T(8,128)(2,1)} %collective-permute-done.13), channel_id=1, source_target_pairs={{0,2},{2,4},{4,6},{6,8},{8,10},{10,12},{12,14},{14,16},{16,18},{18... | collective-permute-start | bytes 589832 | tf_op jit(solution)/shard_map/ppermute | solution.py:15
  180.0 0.6 copy-start
  181.7 3.5 copy-start.1
  185.8 0.6 copy-start.2
  186.5 3.5 copy-start.3
  194.3 0.6 copy-start
  196.0 3.5 copy-start.1
  200.1 0.6 copy-start.2
  200.8 3.5 copy-start.3
  208.6 0.6 copy-start
  210.3 3.5 copy-start.1
  214.5 0.6 copy-start.2
  215.1 3.5 copy-start.3
  235.9 0.6 copy-start
  237.6 3.5 copy-start.1
  241.8 0.6 copy-start.2
  242.4 3.5 copy-start.3
  250.3 0.6 copy-start
  252.0 3.5 copy-start.1
  256.1 0.6 copy-start.2
  256.8 3.5 copy-start.3
  264.6 0.6 copy-start
  266.3 3.5 copy-start.1
  271.1 3.5 copy-start.3
  291.9 0.6 copy-start
  293.6 3.5 copy-start.1
  298.4 3.5 copy-start.3
  306.2 0.6 copy-start
  307.9 3.5 copy-start.1
  312.0 0.6 copy-start.2
  312.7 3.5 copy-start.3
  (2 other events, 1.2 us)
Sparse Core Ops, SparseCore 0:
  65.6 78.8 all-gather.1
  338.4 12.0 reduce-scatter.1
